TPU v7x, 128 devices: a whole 4x4x4 slice. The times are simulated.
128 devices in a mesh: section: 8 (over x, z_hi), dp: 16 (over z_lo, y, core).
Axes of the slice: x: 4, y: 4, z: 4 (z_hi: 2, z_lo: 2; z = z_hi * 2 + z_lo), core: 2. Of those that a mesh axis runs over, the one named last changes fastest.
Arguments:
- inputs: bfloat16 [8, 128, 16384], P(None, None, 'dp'), may hold values from -6 to 6
- cotangent: bfloat16 [8, 8, 128, 1024], P('section'), may hold values from -0.5 to 0.5
- norm_gain: bfloat16 [8, 16384], P('section', 'dp'), may hold values from 0.099609375 to 1.8984375
- value_weight: bfloat16 [8, 16384, 1024], P('section', 'dp'), may hold values from -0.046875 to 0.046875
- output_weight: bfloat16 [8, 1024, 16384], P('section', None, 'dp'), may hold values from -0.1875 to 0.1875
- left_old: float32 [8, 16, 1024, 1024], P('section', 'dp'), may hold values from -0.4 to 2.4, as said below
- right_old: float32 [8, 1024, 1024], P('section', 'dp'), may hold values from -0.4 to 2.4, as said below
Outputs:
- section_outputs: bfloat16 [8, 8, 128, 16384], P('section', None, None, 'dp')
- left_stats: float32 [8, 16, 1024, 1024], P('section', 'dp')
- right_stats: float32 [8, 1024, 1024], P('section', 'dp')
Inputs may be any that keep to these rules, and one draw needn't show every extreme that they name: `left_old`: symmetric in its last two dimensions. `right_old`: symmetric in its last two dimensions.
All inputs are finite; a program needn't handle non-finite values.
Results may differ from a plain program's by a relative error of at most 0.015.
Values may be sent and summed in bfloat16 or wider, within the bound.
A program may use at most 128 MiB of HBM per device.

v0:
```python
import math

import jax
import jax.numpy as jnp
from jax import lax
from jax.sharding import PartitionSpec as P

D = 16384
BLOCK = 1024


def in_blocks(array, dim, size):
    before, after = (array.shape[:dim], array.shape[dim + 1 :])
    return jnp.moveaxis(array.reshape(*before, size, -1, *after), dim, 0)


def sent_and_summed(array, axis, dim):
    tiles = in_blocks(array, dim, lax.axis_size(axis))
    arrived = lax.all_to_all(tiles, axis, split_axis=0, concat_axis=0, tiled=True)
    return arrived.sum(axis=0)


def in_one_piece(arrays, axis, dim, along):
    widths = [math.prod(a.shape[along:]) for a in arrays]
    both = jnp.concatenate(
        [a.reshape(*a.shape[:along], w) for a, w in zip(arrays, widths)], axis=along
    )
    result = sent_and_summed(both, axis, dim)
    tiles = jnp.split(result, [sum(widths[:k]) for k in range(1, len(widths))], axis=along)
    return tuple(
        (b.reshape(*result.shape[:along], *a.shape[along:]) for a, b in zip(arrays, tiles))
    )


def joined_along(tiles, dim):
    tiles = jnp.moveaxis(tiles, 0, dim)
    lengths = tiles.shape
    return tiles.reshape(*lengths[:dim], lengths[dim] * lengths[dim + 1], *lengths[dim + 2 :])


def sent_to_all(array, axis):
    copies = jnp.broadcast_to(array, (lax.axis_size(axis), *array.shape))
    return lax.all_to_all(copies, axis, split_axis=0, concat_axis=0, tiled=True)


def collect(array, axis, dim):
    return joined_along(sent_to_all(array, axis), dim)


def side_by_side(arrays, axis, dim, along):
    widths = [a.shape[along] for a in arrays]
    both = jnp.concatenate(arrays, axis=along)
    result = collect(both, axis, dim)
    return tuple(jnp.split(result, [sum(widths[:k]) for k in range(1, len(widths))], axis=along))


def passed_along(value, axis, steps):
    count = lax.axis_size(axis)
    initial, last = (max(0, -steps), min(count, count - steps))
    return lax.ppermute(value, axis, [(source, source + steps) for source in range(initial, last)])


def summed_on_arrival(array, axis, dim):
    size = lax.axis_size(axis)
    tiles = lax.all_to_all(in_blocks(array, dim, size), axis, 0, 0, tiled=True)
    return jnp.sum(tiles.astype(jnp.float32), axis=0)


def store_slot(buffer, value, position, active):
    before = lax.dynamic_index_in_dim(buffer, position, 0, keepdims=False)
    chosen = jnp.where(active, value, before)
    return lax.dynamic_update_index_in_dim(buffer, chosen, position, 0)


def on_device(inputs, cotangent, norm_gain, value_weight, output_weight, left_old, right_old):
    sections = lax.axis_size("section")
    dp_count = lax.axis_size("dp")
    section_index = lax.axis_index("section")
    owner_index = lax.axis_index("dp")
    micro_count, batch_rows, col_count = inputs.shape
    width_kv = value_weight.shape[2]
    row_share = batch_rows // dp_count
    gain_row = norm_gain[0].astype(jnp.float32)
    w_value = value_weight[0]
    w_output = output_weight[0]
    cotan_all = cotangent[0]
    tick_count = micro_count + sections - 1

    def apply_layer(hidden_in, cotan_rows):
        floats = hidden_in.astype(jnp.float32)
        scaled_in = (floats * gain_row).astype(jnp.bfloat16)
        squares = jnp.sum(floats * floats, axis=1)
        partial_value = jnp.dot(scaled_in, w_value, preferred_element_type=jnp.float32)
        summed, row_total = in_one_piece((partial_value, squares), "dp", 0, 1)
        own_scale = lax.rsqrt(row_total / D + 0.25)
        value_own = (own_scale[:, None] * summed).astype(jnp.bfloat16)
        cotan_own = lax.dynamic_slice_in_dim(cotan_rows, owner_index * row_share, row_share, 0)
        weighted_own = (own_scale[:, None] * cotan_own.astype(jnp.float32)).astype(jnp.bfloat16)
        values, weighted = side_by_side((value_own, weighted_own), "dp", 0, 1)
        result = (floats + jnp.dot(values, w_output, preferred_element_type=jnp.float32)).astype(
            jnp.bfloat16
        )
        return (result, scaled_in, weighted)

    contract_rows = (((0,), (0,)), ((), ()))
    stores = (jnp.zeros((col_count, width_kv), jnp.float32),)
    outputs_init = jnp.zeros((micro_count, batch_rows, col_count), jnp.bfloat16)
    incoming_init = jnp.zeros((batch_rows, col_count), jnp.bfloat16)

    def run_tick(tick_index, state_now):
        incoming, outputs_buf, kept = state_now
        slot_index = tick_index - section_index
        active = (slot_index >= 0) & (slot_index < micro_count)
        position = jnp.clip(slot_index, 0, micro_count - 1)
        entering = lax.dynamic_index_in_dim(
            inputs, jnp.clip(tick_index, 0, micro_count - 1).astype(jnp.int32), 0, keepdims=False
        )
        hidden_in = jnp.where(section_index == 0, entering, incoming)
        cotan_rows = lax.dynamic_index_in_dim(cotan_all, position, 0, keepdims=False)
        result, scaled_in, weighted = apply_layer(hidden_in, cotan_rows)
        outputs_buf = store_slot(outputs_buf, result, position, active)
        update = lax.dot_general(
            scaled_in, weighted, contract_rows, preferred_element_type=jnp.float32
        )
        kept = (kept[0] + jnp.where(active, update, 0.0),)
        incoming = passed_along(result, "section", 1)
        return (incoming, outputs_buf, kept)

    final_state = lax.fori_loop(0, tick_count, run_tick, (incoming_init, outputs_init, stores))
    outputs_buf = final_state[1]
    kept = final_state[2]
    gradient = kept[0]
    grad_half = gradient.astype(jnp.bfloat16)
    blocks = grad_half.reshape(col_count // BLOCK, BLOCK, width_kv)
    left_new = (
        left_old[0]
        + jnp.einsum("bik,bjk->bij", blocks, blocks, preferred_element_type=jnp.float32) / BLOCK
    )
    right_rows = summed_on_arrival(
        lax.dot_general(
            grad_half, grad_half, contract_rows, preferred_element_type=jnp.float32
        ).astype(jnp.bfloat16),
        "dp",
        0,
    )
    right_new = right_old[0] + right_rows / D
    return (outputs_buf[None], left_new[None], right_new[None])


def solution(mesh):
    placed = (
        P(None, None, "dp"),
        P("section", None, None, None),
        P("section", "dp"),
        P("section", "dp", None),
        P("section", None, "dp"),
        P("section", "dp", None, None),
        P("section", "dp", None),
    )
    return jax.shard_map(
        on_device,
        mesh=mesh,
        in_specs=placed,
        out_specs=(
            P("section", None, None, "dp"),
            P("section", "dp", None, None),
            P("section", "dp", None),
        ),
        check_vma=False,
    )
```

profile of v0, /device:TPU:70, one launch (start us, length us, event | category | flops | bytes accessed | tf_op | source)
XLA Modules:
  0.0 767.0 jit_solution(8462426918446477395)
XLA Ops:
  3.1 723.3 %while.21 = (s32[]{:T(128)}, bf16[128,1024]{1,0:T(8,128)(2,1)S(1)}, bf16[8,128,1024]{2,1,0:T(8,128)(2,1)}, f32[1024,1024]{1,0:T(8,128)}, pred[]{:T(512)}, /*inde...) while((s32[]{:T(128)}, bf16[128,1024]{1,0:T(8,128)(2,1)S(1)}, ...), condition=%wide.region_3.4_spmd.clone, body=%wide.region_0.3_spmd.clone.sunk | while | flops 810647680 | bytes 23162892 | solution.py:129
  13.0 11.5 %all-to-all-done = f32[16,8,1025]{2,1,0:T(8,128)S(1)} async-done(((f32[16,8,1025]{2,1,0:T(8,128)}), f32[16,8,1025]{2,1,0:T(8,128)S(1)}, u32[]{:S(2)}, u32[]{:S(2)}) %all-to-all-start) | async-done | bytes 524832 | tf_op jit(solution)/shard_map/while/body/eval_jaxpr/all_to_all | solution.py:19
  30.9 9.8 %all-to-all-done.1 = bf16[16,8,2048]{2,1,0:T(8,128)(2,1)S(1)} async-done(((bf16[16,8,2048]{2,1,0:T(8,128)(2,1)}), bf16[16,8,2048]{2,1,0:T(8,128)(2,1)S(1)}, u32[]{:S(2)}, u32[]{:S(2)}) %all-to-all-start.1) | async-done | bytes 524320 | tf_op jit(solution)/shard_map/while/body/eval_jaxpr/all_to_all | solution.py:43
  60.5 11.5 %all-to-all-done = f32[16,8,1025]{2,1,0:T(8,128)S(1)} async-done(((f32[16,8,1025]{2,1,0:T(8,128)}), f32[16,8,1025]{2,1,0:T(8,128)S(1)}, u32[]{:S(2)}, u32[]{:S(2)}) %all-to-all-start) | async-done | bytes 524832 | tf_op jit(solution)/shard_map/while/body/eval_jaxpr/all_to_all | solution.py:19
  78.4 9.8 %all-to-all-done.1 = bf16[16,8,2048]{2,1,0:T(8,128)(2,1)S(1)} async-done(((bf16[16,8,2048]{2,1,0:T(8,128)(2,1)}), bf16[16,8,2048]{2,1,0:T(8,128)(2,1)S(1)}, u32[]{:S(2)}, u32[]{:S(2)}) %all-to-all-start.1) | async-done | bytes 524320 | tf_op jit(solution)/shard_map/while/body/eval_jaxpr/all_to_all | solution.py:43
  107.9 11.5 %all-to-all-done = f32[16,8,1025]{2,1,0:T(8,128)S(1)} async-done(((f32[16,8,1025]{2,1,0:T(8,128)}), f32[16,8,1025]{2,1,0:T(8,128)S(1)}, u32[]{:S(2)}, u32[]{:S(2)}) %all-to-all-start) | async-done | bytes 524832 | tf_op jit(solution)/shard_map/while/body/eval_jaxpr/all_to_all | solution.py:19
  155.4 11.5 %all-to-all-done = f32[16,8,1025]{2,1,0:T(8,128)S(1)} async-done(((f32[16,8,1025]{2,1,0:T(8,128)}), f32[16,8,1025]{2,1,0:T(8,128)S(1)}, u32[]{:S(2)}, u32[]{:S(2)}) %all-to-all-start) | async-done | bytes 524832 | tf_op jit(solution)/shard_map/while/body/eval_jaxpr/all_to_all | solution.py:19
  173.3 9.8 %all-to-all-done.1 = bf16[16,8,2048]{2,1,0:T(8,128)(2,1)S(1)} async-done(((bf16[16,8,2048]{2,1,0:T(8,128)(2,1)}), bf16[16,8,2048]{2,1,0:T(8,128)(2,1)S(1)}, u32[]{:S(2)}, u32[]{:S(2)}) %all-to-all-start.1) | async-done | bytes 524320 | tf_op jit(solution)/shard_map/while/body/eval_jaxpr/all_to_all | solution.py:43
  202.9 11.5 %all-to-all-done = f32[16,8,1025]{2,1,0:T(8,128)S(1)} async-done(((f32[16,8,1025]{2,1,0:T(8,128)}), f32[16,8,1025]{2,1,0:T(8,128)S(1)}, u32[]{:S(2)}, u32[]{:S(2)}) %all-to-all-start) | async-done | bytes 524832 | tf_op jit(solution)/shard_map/while/body/eval_jaxpr/all_to_all | solution.py:19
  220.8 9.8 %all-to-all-done.1 = bf16[16,8,2048]{2,1,0:T(8,128)(2,1)S(1)} async-done(((bf16[16,8,2048]{2,1,0:T(8,128)(2,1)}), bf16[16,8,2048]{2,1,0:T(8,128)(2,1)S(1)}, u32[]{:S(2)}, u32[]{:S(2)}) %all-to-all-start.1) | async-done | bytes 524320 | tf_op jit(solution)/shard_map/while/body/eval_jaxpr/all_to_all | solution.py:43
  251.2 11.5 %all-to-all-done = f32[16,8,1025]{2,1,0:T(8,128)S(1)} async-done(((f32[16,8,1025]{2,1,0:T(8,128)}), f32[16,8,1025]{2,1,0:T(8,128)S(1)}, u32[]{:S(2)}, u32[]{:S(2)}) %all-to-all-start) | async-done | bytes 524832 | tf_op jit(solution)/shard_map/while/body/eval_jaxpr/all_to_all | solution.py:19
  269.2 9.8 %all-to-all-done.1 = bf16[16,8,2048]{2,1,0:T(8,128)(2,1)S(1)} async-done(((bf16[16,8,2048]{2,1,0:T(8,128)(2,1)}), bf16[16,8,2048]{2,1,0:T(8,128)(2,1)S(1)}, u32[]{:S(2)}, u32[]{:S(2)}) %all-to-all-start.1) | async-done | bytes 524320 | tf_op jit(solution)/shard_map/while/body/eval_jaxpr/all_to_all | solution.py:43
  299.6 11.5 %all-to-all-done = f32[16,8,1025]{2,1,0:T(8,128)S(1)} async-done(((f32[16,8,1025]{2,1,0:T(8,128)}), f32[16,8,1025]{2,1,0:T(8,128)S(1)}, u32[]{:S(2)}, u32[]{:S(2)}) %all-to-all-start) | async-done | bytes 524832 | tf_op jit(solution)/shard_map/while/body/eval_jaxpr/all_to_all | solution.py:19
  348.0 11.5 %all-to-all-done = f32[16,8,1025]{2,1,0:T(8,128)S(1)} async-done(((f32[16,8,1025]{2,1,0:T(8,128)}), f32[16,8,1025]{2,1,0:T(8,128)S(1)}, u32[]{:S(2)}, u32[]{:S(2)}) %all-to-all-start) | async-done | bytes 524832 | tf_op jit(solution)/shard_map/while/body/eval_jaxpr/all_to_all | solution.py:19
  396.3 11.5 %all-to-all-done = f32[16,8,1025]{2,1,0:T(8,128)S(1)} async-done(((f32[16,8,1025]{2,1,0:T(8,128)}), f32[16,8,1025]{2,1,0:T(8,128)S(1)}, u32[]{:S(2)}, u32[]{:S(2)}) %all-to-all-start) | async-done | bytes 524832 | tf_op jit(solution)/shard_map/while/body/eval_jaxpr/all_to_all | solution.py:19
  414.3 9.8 %all-to-all-done.1 = bf16[16,8,2048]{2,1,0:T(8,128)(2,1)S(1)} async-done(((bf16[16,8,2048]{2,1,0:T(8,128)(2,1)}), bf16[16,8,2048]{2,1,0:T(8,128)(2,1)S(1)}, u32[]{:S(2)}, u32[]{:S(2)}) %all-to-all-start.1) | async-done | bytes 524320 | tf_op jit(solution)/shard_map/while/body/eval_jaxpr/all_to_all | solution.py:43
  444.7 11.5 %all-to-all-done = f32[16,8,1025]{2,1,0:T(8,128)S(1)} async-done(((f32[16,8,1025]{2,1,0:T(8,128)}), f32[16,8,1025]{2,1,0:T(8,128)S(1)}, u32[]{:S(2)}, u32[]{:S(2)}) %all-to-all-start) | async-done | bytes 524832 | tf_op jit(solution)/shard_map/while/body/eval_jaxpr/all_to_all | solution.py:19
  462.6 9.8 %all-to-all-done.1 = bf16[16,8,2048]{2,1,0:T(8,128)(2,1)S(1)} async-done(((bf16[16,8,2048]{2,1,0:T(8,128)(2,1)}), bf16[16,8,2048]{2,1,0:T(8,128)(2,1)S(1)}, u32[]{:S(2)}, u32[]{:S(2)}) %all-to-all-start.1) | async-done | bytes 524320 | tf_op jit(solution)/shard_map/while/body/eval_jaxpr/all_to_all | solution.py:43
  493.0 11.5 %all-to-all-done = f32[16,8,1025]{2,1,0:T(8,128)S(1)} async-done(((f32[16,8,1025]{2,1,0:T(8,128)}), f32[16,8,1025]{2,1,0:T(8,128)S(1)}, u32[]{:S(2)}, u32[]{:S(2)}) %all-to-all-start) | async-done | bytes 524832 | tf_op jit(solution)/shard_map/while/body/eval_jaxpr/all_to_all | solution.py:19
  541.4 11.5 %all-to-all-done = f32[16,8,1025]{2,1,0:T(8,128)S(1)} async-done(((f32[16,8,1025]{2,1,0:T(8,128)}), f32[16,8,1025]{2,1,0:T(8,128)S(1)}, u32[]{:S(2)}, u32[]{:S(2)}) %all-to-all-start) | async-done | bytes 524832 | tf_op jit(solution)/shard_map/while/body/eval_jaxpr/all_to_all | solution.py:19
  589.8 11.5 %all-to-all-done = f32[16,8,1025]{2,1,0:T(8,128)S(1)} async-done(((f32[16,8,1025]{2,1,0:T(8,128)}), f32[16,8,1025]{2,1,0:T(8,128)S(1)}, u32[]{:S(2)}, u32[]{:S(2)}) %all-to-all-start) | async-done | bytes 524832 | tf_op jit(solution)/shard_map/while/body/eval_jaxpr/all_to_all | solution.py:19
  638.1 11.5 %all-to-all-done = f32[16,8,1025]{2,1,0:T(8,128)S(1)} async-done(((f32[16,8,1025]{2,1,0:T(8,128)}), f32[16,8,1025]{2,1,0:T(8,128)S(1)}, u32[]{:S(2)}, u32[]{:S(2)}) %all-to-all-start) | async-done | bytes 524832 | tf_op jit(solution)/shard_map/while/body/eval_jaxpr/all_to_all | solution.py:19
  686.5 11.5 %all-to-all-done = f32[16,8,1025]{2,1,0:T(8,128)S(1)} async-done(((f32[16,8,1025]{2,1,0:T(8,128)}), f32[16,8,1025]{2,1,0:T(8,128)S(1)}, u32[]{:S(2)}, u32[]{:S(2)}) %all-to-all-start) | async-done | bytes 524832 | tf_op jit(solution)/shard_map/while/body/eval_jaxpr/all_to_all | solution.py:19
  746.8 19.0 %all-to-all-done.2 = bf16[16,64,1024]{2,1,0:T(8,128)(2,1)S(1)} async-done(((bf16[16,64,1024]{2,1,0:T(8,128)(2,1)}), bf16[16,64,1024]{2,1,0:T(8,128)(2,1)S(1)}, u32[]{:S(2)}, u32[]{:S(2)}) %all-to-all-start.2) | async-done | bytes 2097184 | tf_op jit(solution)/shard_map/all_to_all | solution.py:65
  (261 shorter events, 504.8 us)
Async XLA Ops:
  7.3 17.2 %all-to-all-start = ((f32[16,8,1025]{2,1,0:T(8,128)}), f32[16,8,1025]{2,1,0:T(8,128)S(1)}, u32[]{:S(2)}, u32[]{:S(2)}) async-start(f32[16,8,1025]{2,1,0:T(8,128)} %pad_maximum_fusion.4), calls=%async_computation | async-start | bytes 1179648 | tf_op jit(solution)/shard_map/while/body/eval_jaxpr/all_to_all | solution.py:19
  26.4 14.4 %all-to-all-start.1 = ((bf16[16,8,2048]{2,1,0:T(8,128)(2,1)}), bf16[16,8,2048]{2,1,0:T(8,128)(2,1)S(1)}, u32[]{:S(2)}, u32[]{:S(2)}) async-start(bf16[16,8,2048]{2,1,0:T(8,128)(2,1)} %broadcast_in_dim.67), calls=%async_computation.1 | async-start | bytes 1048576 | tf_op jit(solution)/shard_map/while/body/eval_jaxpr/all_to_all | solution.py:43
  56.9 15.1 %all-to-all-start = ((f32[16,8,1025]{2,1,0:T(8,128)}), f32[16,8,1025]{2,1,0:T(8,128)S(1)}, u32[]{:S(2)}, u32[]{:S(2)}) async-start(f32[16,8,1025]{2,1,0:T(8,128)} %pad_maximum_fusion.4), calls=%async_computation | async-start | bytes 1179648 | tf_op jit(solution)/shard_map/while/body/eval_jaxpr/all_to_all | solution.py:19
  73.8 14.4 %all-to-all-start.1 = ((bf16[16,8,2048]{2,1,0:T(8,128)(2,1)}), bf16[16,8,2048]{2,1,0:T(8,128)(2,1)S(1)}, u32[]{:S(2)}, u32[]{:S(2)}) async-start(bf16[16,8,2048]{2,1,0:T(8,128)(2,1)} %broadcast_in_dim.67), calls=%async_computation.1 | async-start | bytes 1048576 | tf_op jit(solution)/shard_map/while/body/eval_jaxpr/all_to_all | solution.py:43
  104.3 15.1 %all-to-all-start = ((f32[16,8,1025]{2,1,0:T(8,128)}), f32[16,8,1025]{2,1,0:T(8,128)S(1)}, u32[]{:S(2)}, u32[]{:S(2)}) async-start(f32[16,8,1025]{2,1,0:T(8,128)} %pad_maximum_fusion.4), calls=%async_computation | async-start | bytes 1179648 | tf_op jit(solution)/shard_map/while/body/eval_jaxpr/all_to_all | solution.py:19
  121.3 14.4 %all-to-all-start.1 = ((bf16[16,8,2048]{2,1,0:T(8,128)(2,1)}), bf16[16,8,2048]{2,1,0:T(8,128)(2,1)S(1)}, u32[]{:S(2)}, u32[]{:S(2)}) async-start(bf16[16,8,2048]{2,1,0:T(8,128)(2,1)} %broadcast_in_dim.67), calls=%async_computation.1 | async-start | bytes 1048576 | tf_op jit(solution)/shard_map/while/body/eval_jaxpr/all_to_all | solution.py:43
  151.8 15.1 %all-to-all-start = ((f32[16,8,1025]{2,1,0:T(8,128)}), f32[16,8,1025]{2,1,0:T(8,128)S(1)}, u32[]{:S(2)}, u32[]{:S(2)}) async-start(f32[16,8,1025]{2,1,0:T(8,128)} %pad_maximum_fusion.4), calls=%async_computation | async-start | bytes 1179648 | tf_op jit(solution)/shard_map/while/body/eval_jaxpr/all_to_all | solution.py:19
  168.8 14.4 %all-to-all-start.1 = ((bf16[16,8,2048]{2,1,0:T(8,128)(2,1)}), bf16[16,8,2048]{2,1,0:T(8,128)(2,1)S(1)}, u32[]{:S(2)}, u32[]{:S(2)}) async-start(bf16[16,8,2048]{2,1,0:T(8,128)(2,1)} %broadcast_in_dim.67), calls=%async_computation.1 | async-start | bytes 1048576 | tf_op jit(solution)/shard_map/while/body/eval_jaxpr/all_to_all | solution.py:43
  199.3 15.1 %all-to-all-start = ((f32[16,8,1025]{2,1,0:T(8,128)}), f32[16,8,1025]{2,1,0:T(8,128)S(1)}, u32[]{:S(2)}, u32[]{:S(2)}) async-start(f32[16,8,1025]{2,1,0:T(8,128)} %pad_maximum_fusion.4), calls=%async_computation | async-start | bytes 1179648 | tf_op jit(solution)/shard_map/while/body/eval_jaxpr/all_to_all | solution.py:19
  216.2 14.4 %all-to-all-start.1 = ((bf16[16,8,2048]{2,1,0:T(8,128)(2,1)}), bf16[16,8,2048]{2,1,0:T(8,128)(2,1)S(1)}, u32[]{:S(2)}, u32[]{:S(2)}) async-start(bf16[16,8,2048]{2,1,0:T(8,128)(2,1)} %broadcast_in_dim.67), calls=%async_computation.1 | async-start | bytes 1048576 | tf_op jit(solution)/shard_map/while/body/eval_jaxpr/all_to_all | solution.py:43
  247.0 15.7 %all-to-all-start = ((f32[16,8,1025]{2,1,0:T(8,128)}), f32[16,8,1025]{2,1,0:T(8,128)S(1)}, u32[]{:S(2)}, u32[]{:S(2)}) async-start(f32[16,8,1025]{2,1,0:T(8,128)} %pad_maximum_fusion.4), calls=%async_computation | async-start | bytes 1179648 | tf_op jit(solution)/shard_map/while/body/eval_jaxpr/all_to_all | solution.py:19
  264.6 14.4 %all-to-all-start.1 = ((bf16[16,8,2048]{2,1,0:T(8,128)(2,1)}), bf16[16,8,2048]{2,1,0:T(8,128)(2,1)S(1)}, u32[]{:S(2)}, u32[]{:S(2)}) async-start(bf16[16,8,2048]{2,1,0:T(8,128)(2,1)} %broadcast_in_dim.67), calls=%async_computation.1 | async-start | bytes 1048576 | tf_op jit(solution)/shard_map/while/body/eval_jaxpr/all_to_all | solution.py:43
  295.4 15.7 %all-to-all-start = ((f32[16,8,1025]{2,1,0:T(8,128)}), f32[16,8,1025]{2,1,0:T(8,128)S(1)}, u32[]{:S(2)}, u32[]{:S(2)}) async-start(f32[16,8,1025]{2,1,0:T(8,128)} %pad_maximum_fusion.4), calls=%async_computation | async-start | bytes 1179648 | tf_op jit(solution)/shard_map/while/body/eval_jaxpr/all_to_all | solution.py:19
  313.0 14.4 %all-to-all-start.1 = ((bf16[16,8,2048]{2,1,0:T(8,128)(2,1)}), bf16[16,8,2048]{2,1,0:T(8,128)(2,1)S(1)}, u32[]{:S(2)}, u32[]{:S(2)}) async-start(bf16[16,8,2048]{2,1,0:T(8,128)(2,1)} %broadcast_in_dim.67), calls=%async_computation.1 | async-start | bytes 1048576 | tf_op jit(solution)/shard_map/while/body/eval_jaxpr/all_to_all | solution.py:43
  343.8 15.7 %all-to-all-start = ((f32[16,8,1025]{2,1,0:T(8,128)}), f32[16,8,1025]{2,1,0:T(8,128)S(1)}, u32[]{:S(2)}, u32[]{:S(2)}) async-start(f32[16,8,1025]{2,1,0:T(8,128)} %pad_maximum_fusion.4), calls=%async_computation | async-start | bytes 1179648 | tf_op jit(solution)/shard_map/while/body/eval_jaxpr/all_to_all | solution.py:19
  392.1 15.7 %all-to-all-start = ((f32[16,8,1025]{2,1,0:T(8,128)}), f32[16,8,1025]{2,1,0:T(8,128)S(1)}, u32[]{:S(2)}, u32[]{:S(2)}) async-start(f32[16,8,1025]{2,1,0:T(8,128)} %pad_maximum_fusion.4), calls=%async_computation | async-start | bytes 1179648 | tf_op jit(solution)/shard_map/while/body/eval_jaxpr/all_to_all | solution.py:19
  409.7 14.4 %all-to-all-start.1 = ((bf16[16,8,2048]{2,1,0:T(8,128)(2,1)}), bf16[16,8,2048]{2,1,0:T(8,128)(2,1)S(1)}, u32[]{:S(2)}, u32[]{:S(2)}) async-start(bf16[16,8,2048]{2,1,0:T(8,128)(2,1)} %broadcast_in_dim.67), calls=%async_computation.1 | async-start | bytes 1048576 | tf_op jit(solution)/shard_map/while/body/eval_jaxpr/all_to_all | solution.py:43
  440.5 15.7 %all-to-all-start = ((f32[16,8,1025]{2,1,0:T(8,128)}), f32[16,8,1025]{2,1,0:T(8,128)S(1)}, u32[]{:S(2)}, u32[]{:S(2)}) async-start(f32[16,8,1025]{2,1,0:T(8,128)} %pad_maximum_fusion.4), calls=%async_computation | async-start | bytes 1179648 | tf_op jit(solution)/shard_map/while/body/eval_jaxpr/all_to_all | solution.py:19
  488.8 15.7 %all-to-all-start = ((f32[16,8,1025]{2,1,0:T(8,128)}), f32[16,8,1025]{2,1,0:T(8,128)S(1)}, u32[]{:S(2)}, u32[]{:S(2)}) async-start(f32[16,8,1025]{2,1,0:T(8,128)} %pad_maximum_fusion.4), calls=%async_computation | async-start | bytes 1179648 | tf_op jit(solution)/shard_map/while/body/eval_jaxpr/all_to_all | solution.py:19
  537.2 15.7 %all-to-all-start = ((f32[16,8,1025]{2,1,0:T(8,128)}), f32[16,8,1025]{2,1,0:T(8,128)S(1)}, u32[]{:S(2)}, u32[]{:S(2)}) async-start(f32[16,8,1025]{2,1,0:T(8,128)} %pad_maximum_fusion.4), calls=%async_computation | async-start | bytes 1179648 | tf_op jit(solution)/shard_map/while/body/eval_jaxpr/all_to_all | solution.py:19
  585.6 15.7 %all-to-all-start = ((f32[16,8,1025]{2,1,0:T(8,128)}), f32[16,8,1025]{2,1,0:T(8,128)S(1)}, u32[]{:S(2)}, u32[]{:S(2)}) async-start(f32[16,8,1025]{2,1,0:T(8,128)} %pad_maximum_fusion.4), calls=%async_computation | async-start | bytes 1179648 | tf_op jit(solution)/shard_map/while/body/eval_jaxpr/all_to_all | solution.py:19
  633.9 15.7 %all-to-all-start = ((f32[16,8,1025]{2,1,0:T(8,128)}), f32[16,8,1025]{2,1,0:T(8,128)S(1)}, u32[]{:S(2)}, u32[]{:S(2)}) async-start(f32[16,8,1025]{2,1,0:T(8,128)} %pad_maximum_fusion.4), calls=%async_computation | async-start | bytes 1179648 | tf_op jit(solution)/shard_map/while/body/eval_jaxpr/all_to_all | solution.py:19
  682.3 15.7 %all-to-all-start = ((f32[16,8,1025]{2,1,0:T(8,128)}), f32[16,8,1025]{2,1,0:T(8,128)S(1)}, u32[]{:S(2)}, u32[]{:S(2)}) async-start(f32[16,8,1025]{2,1,0:T(8,128)} %pad_maximum_fusion.4), calls=%async_computation | async-start | bytes 1179648 | tf_op jit(solution)/shard_map/while/body/eval_jaxpr/all_to_all | solution.py:19
  733.6 32.3 %all-to-all-start.2 = ((bf16[16,64,1024]{2,1,0:T(8,128)(2,1)}), bf16[16,64,1024]{2,1,0:T(8,128)(2,1)S(1)}, u32[]{:S(2)}, u32[]{:S(2)}) async-start(bf16[16,64,1024]{2,1,0:T(8,128)(2,1)} %bitcast.48), calls=%async_computation.2 | async-start | bytes 4194304 | tf_op jit(solution)/shard_map/all_to_all | solution.py:65
  (24 other events, 286.1 us)
where the time goes:
time: 778 us; the launch traced here: 767 us
  waiting for transfers between devices  412 us (53%)
  starting transfers between devices  139 us (18%)
  matrix products  136 us (17%)
  other arithmetic  46.8 us (6%)
  local copies, waits for them, and re-layouts  31.9 us (4%)
    all_to_all x15, waiting for transfers between devices, sent_and_summed(): lax.all_to_all(tiles, axis, split_axis=0, concat_axis=0, tiled=True)  173 us
    all_to_all x15, waiting for transfers between devices, sent_to_all(): return lax.all_to_all(copies, axis, split_axis=0, concat_axis=0, tiled=True)  147 us
    ppermute x15, waiting for transfers between devices, passed_along(): lax.ppermute(value, axis, [(source, source + steps) for source in range(i...  73.3 us
    dot_general x15, matrix products, run_tick(): lax.dot_general(scaled_in, weighted, contract_rows, preferred_element_typ...  70.9 us
    all_to_all x15, starting transfers between devices, sent_and_summed(): lax.all_to_all(tiles, axis, split_axis=0, concat_axis=0, tiled=True)  61.8 us
    all_to_all x15, starting transfers between devices, sent_to_all(): return lax.all_to_all(copies, axis, split_axis=0, concat_axis=0, tiled=True)  53.6 us
    dot_general x15, matrix products, apply_layer(): jnp.dot(scaled_in, w_value, preferred_element_type=jnp.float32)  30.5 us
    ppermute x15, starting transfers between devices, passed_along(): lax.ppermute(value, axis, [(source, source + steps) for source in range(i...  19.2 us
  transfers between devices with their start and end apart: 46, of which 46 were waited for; matrix products, arithmetic and copies ran while one was open for 12% of the time, Pallas kernels for 0%

commit v1 on v0

v1 whole, which is shorter than its diff:
```python
import jax
import jax.numpy as jnp
from jax import lax
from jax.experimental import pallas as pl
from jax.experimental.pallas import tpu as pltpu
from jax.sharding import PartitionSpec as P

MESH = pl.DeviceIdType.MESH
F32 = jnp.float32
BF16 = jnp.bfloat16

D = 16384
W = 1024
KV = 1024
ROWS = 1024
T = 64
NC = ROWS // T
PLANE = 8
OWN = T // PLANE
EXT = KV + 128
Y = 4


def with_pair(rows, scalar):
    high = scalar.astype(BF16).astype(F32)
    low = scalar - high
    lane = lax.broadcasted_iota(jnp.int32, (rows.shape[0], 128), 1)
    pair = jnp.where(lane < 64, high, low)
    return jnp.concatenate([rows, pair], axis=1)


def pair_of(ext):
    return ext[:, KV : KV + 1] + ext[:, KV + 64 : KV + 65]


def kernel(
    x_hbm, cot_hbm, gain_ref, wv_hbm, wo_hbm, left_old_hbm, right_old_hbm,
    out_hbm, left_hbm, right_hbm,
    wv, wo, cot, xbuf, sc, outbuf, part, rs, zs, zr, val, wgt, gb, left, right,
    rp, r1, r1s, r2, r2s, r3,
    load_sem, x_sem, xsend_sem, rs_sem, rssend_sem, z_sem, zsend_sem, ag_sem, agsend_sem,
    out_sem, r_sem, rsend_sem,
):
    s = lax.axis_index("section")
    d = lax.axis_index("dp")
    p = lax.rem(d, PLANE)
    zl = d // PLANE
    core = lax.rem(d, 2)
    y = p // 2
    zpeer = (s, lax.rem(d + PLANE, 2 * PLANE))
    cpeer = (s, d + 1 - 2 * core)

    def plane_peer(offset):
        return (s, zl * PLANE + lax.rem(p + offset, PLANE))

    load_wv = pltpu.make_async_copy(wv_hbm, wv, load_sem.at[0])
    load_wo = pltpu.make_async_copy(wo_hbm, wo, load_sem.at[1])
    load_cot = pltpu.make_async_copy(cot_hbm, cot, load_sem.at[2])
    load_left = pltpu.make_async_copy(left_old_hbm, left, load_sem.at[3])
    load_right = pltpu.make_async_copy(right_old_hbm, right, load_sem.at[4])
    load_wv.start()

    @pl.when(s == 0)
    def _():
        def body(c, carry):
            pltpu.make_async_copy(x_hbm.at[c], xbuf.at[c], x_sem.at[c]).start()
            return carry

        lax.fori_loop(0, NC, body, 0)

    load_wo.start()
    load_cot.start()
    load_left.start()
    load_right.start()

    barrier = pltpu.get_barrier_semaphore()
    for offset in range(1, PLANE):
        pl.semaphore_signal(barrier, inc=1, device_id=plane_peer(offset), device_id_type=MESH)
    pl.semaphore_signal(barrier, inc=1, device_id=zpeer, device_id_type=MESH)

    for step in (1, 7):
        pl.semaphore_signal(
            barrier, inc=1, device_id=(lax.rem(s + step, 8), d), device_id_type=MESH
        )
    pl.semaphore_wait(barrier, PLANE + 2)
    load_wv.wait()
    load_wo.wait()
    load_cot.wait()

    def rs_copy(c, offset):
        return pltpu.make_async_remote_copy(
            src_ref=part.at[c, lax.rem(p + offset, PLANE)],
            dst_ref=rs.at[c, offset - 1],
            send_sem=rssend_sem.at[c],
            recv_sem=rs_sem.at[c],
            device_id=plane_peer(offset),
            device_id_type=MESH,
        )

    def z_copy(c):
        return pltpu.make_async_remote_copy(
            src_ref=zs.at[c], dst_ref=zr.at[c], send_sem=zsend_sem.at[c], recv_sem=z_sem.at[c],
            device_id=zpeer, device_id_type=MESH,
        )

    def ag_copy(c, offset):
        return pltpu.make_async_remote_copy(
            src_ref=val.at[c, p], dst_ref=val.at[c, p], send_sem=agsend_sem.at[c], recv_sem=ag_sem.at[c],
            device_id=plane_peer(offset), device_id_type=MESH,
        )

    def x_copy(c):
        return pltpu.make_async_remote_copy(
            src_ref=outbuf.at[c], dst_ref=xbuf.at[c], send_sem=xsend_sem.at[c], recv_sem=x_sem.at[c],
            device_id=(s + 1, d), device_id_type=MESH,
        )

    def out_copy(c):
        return pltpu.make_async_copy(outbuf.at[c], out_hbm.at[c], out_sem.at[c])

    def tick(k, carry):
        @pl.when(k < NC)
        def _():
            c = k
            pltpu.make_async_copy(x_hbm.at[c], xbuf.at[c], x_sem.at[c]).wait()
            floats = xbuf[c].astype(F32)
            scaled = (floats * gain_ref[...].astype(F32)).astype(BF16)
            sc[pl.ds(pl.multiple_of(c * T, T), T), :] = scaled
            squares = jnp.sum(floats * floats, axis=1, keepdims=True)
            product = jnp.dot(scaled, wv[...], preferred_element_type=F32)
            both = with_pair(product, squares)
            part[c] = both.reshape(PLANE, OWN, EXT).astype(BF16)
            for offset in range(1, PLANE):
                rs_copy(c, offset).start()

        @pl.when((k >= 1) & (k <= NC))
        def _():
            c = k - 1
            pltpu.make_async_copy(rs.at[c], rs.at[c], rs_sem.at[c]).wait()
            total = part[c, p].astype(F32)
            for j in range(PLANE - 1):
                total += rs[c, j].astype(F32)
            mine = with_pair(total[:, :KV], pair_of(total)).astype(BF16)
            zs[c] = mine
            z_copy(c).start()
            pltpu.make_async_copy(zr.at[c], zr.at[c], z_sem.at[c]).wait()
            total = zs[c].astype(F32) + zr[c].astype(F32)
            inv = lax.rsqrt(pair_of(total) / D + 0.25)
            val[c, p] = with_pair(inv * total[:, :KV], inv).astype(BF16)
            for offset in range(1, PLANE):
                ag_copy(c, offset).start()

        @pl.when(k >= 2)
        def _():
            c = k - 2
            pltpu.make_async_copy(rs.at[c], rs.at[c], ag_sem.at[c]).wait()
            rows = pl.ds(pl.multiple_of(c * T, T), T)
            both = val[c].astype(F32).reshape(T, EXT)
            values = both[:, :KV].astype(BF16)
            result = xbuf[c].astype(F32) + jnp.dot(values, wo[...], preferred_element_type=F32)
            outbuf[c] = result.astype(BF16)

            @pl.when(s < 7)
            def _():
                x_copy(c).start()

            out_copy(c).start()
            wgt[rows, :] = (pair_of(both) * cot[rows, :].astype(F32)).astype(BF16)

        return carry

    lax.fori_loop(0, NC + 2, tick, 0)

    over_rows = (((0,), (0,)), ((), ()))
    over_cols = (((1,), (1,)), ((), ()))
    STEP = 256

    def block(i):
        return pl.ds(pl.multiple_of(i * STEP, STEP), STEP)

    def grad_block(i, carry):
        gb[block(i), :] = lax.dot_general(
            sc[:, block(i)], wgt[...], over_rows, preferred_element_type=F32
        ).astype(BF16)
        return carry

    lax.fori_loop(0, W // STEP, grad_block, 0)

    def right_block(i, carry):
        rows = lax.dot_general(gb[:, block(i)], gb[...], over_rows, preferred_element_type=F32).astype(BF16)
        for j in range(4):
            rp[j % 2, 2 * lax.rem(i, 2) + j // 2, i // 2] = rows[64 * j : 64 * (j + 1), :]
        return carry

    lax.fori_loop(0, KV // STEP, right_block, 0)

    core_copy = pltpu.make_async_remote_copy(
        src_ref=rp.at[1 - core], dst_ref=r1, send_sem=rsend_sem.at[0], recv_sem=r_sem.at[0],
        device_id=cpeer, device_id_type=MESH,
    )
    core_copy.start()

    load_left.wait()
    load_right.wait()

    def left_block(i, carry):
        add = lax.dot_general(gb[block(i), :], gb[...], over_cols, preferred_element_type=F32)
        left[block(i), :] = left[block(i), :] + add * (1.0 / 1024)
        return carry

    lax.fori_loop(0, 2, left_block, 0)
    core_copy.wait()
    r1s[...] = (rp[core].astype(F32) + r1[...].astype(F32)).astype(BF16)

    def y_copy(offset):
        return pltpu.make_async_remote_copy(
            src_ref=r1s.at[lax.rem(y + offset, Y)], dst_ref=r2.at[offset - 1],
            send_sem=rsend_sem.at[1], recv_sem=r_sem.at[1],
            device_id=(s, zl * PLANE + lax.rem(y + offset, Y) * 2 + core), device_id_type=MESH,
        )

    for offset in range(1, Y):
        y_copy(offset).start()
    lax.fori_loop(2, 4, left_block, 0)
    left_copy = pltpu.make_async_copy(left, left_hbm, load_sem.at[3])
    left_copy.start()
    pltpu.make_async_copy(r2, r2, r_sem.at[1]).wait()
    summed = r1s[y].astype(F32)
    for j in range(Y - 1):
        summed += r2[j].astype(F32)
    r2s[...] = summed.astype(BF16)
    last_copy = pltpu.make_async_remote_copy(
        src_ref=r2s.at[1 - zl], dst_ref=r3, send_sem=rsend_sem.at[2], recv_sem=r_sem.at[2],
        device_id=zpeer, device_id_type=MESH,
    )
    last_copy.start()
    last_copy.wait()
    right[...] = right[...] + (r2s[zl].astype(F32) + r3[...].astype(F32)) * (1.0 / D)
    right_copy = pltpu.make_async_copy(right, right_hbm, load_sem.at[4])
    right_copy.start()

    pltpu.make_async_copy(r2, r2, rsend_sem.at[1]).wait()

    def drain(c, carry):
        pltpu.make_async_copy(rs.at[c], rs.at[c], rssend_sem.at[c]).wait()
        pltpu.make_async_copy(rs.at[c], rs.at[c], agsend_sem.at[c]).wait()
        pltpu.make_async_copy(zs.at[c], zs.at[c], zsend_sem.at[c]).wait()
        out_copy(c).wait()

        @pl.when(s < 7)
        def _():
            pltpu.make_async_copy(outbuf.at[c], outbuf.at[c], xsend_sem.at[c]).wait()

        return carry

    lax.fori_loop(0, NC, drain, 0)
    left_copy.wait()
    right_copy.wait()


def on_device(inputs, cotangent, norm_gain, value_weight, output_weight, left_old, right_old):
    any_space = pl.BlockSpec(memory_space=pl.ANY)
    vmem = pl.BlockSpec(memory_space=pltpu.VMEM)
    dma = pltpu.SemaphoreType.DMA
    out, left, right = pl.pallas_call(
        kernel,
        out_shape=(
            jax.ShapeDtypeStruct((NC, T, W), BF16),
            jax.ShapeDtypeStruct((W, W), F32),
            jax.ShapeDtypeStruct((64, KV), F32),
        ),
        in_specs=[any_space, any_space, vmem, any_space, any_space, any_space, any_space],
        out_specs=(any_space, any_space, any_space),
        scratch_shapes=[
            pltpu.VMEM((W, KV), BF16),
            pltpu.VMEM((KV, W), BF16),
            pltpu.VMEM((ROWS, KV), BF16),
            pltpu.VMEM((NC, T, W), BF16),
            pltpu.VMEM((ROWS, W), BF16),
            pltpu.VMEM((NC, T, W), BF16),
            pltpu.VMEM((NC, PLANE, OWN, EXT), BF16),
            pltpu.VMEM((NC, PLANE - 1, OWN, EXT), BF16),
            pltpu.VMEM((NC, OWN, EXT), BF16),
            pltpu.VMEM((NC, OWN, EXT), BF16),
            pltpu.VMEM((NC, PLANE, OWN, EXT), BF16),
            pltpu.VMEM((ROWS, KV), BF16),
            pltpu.VMEM((W, KV), BF16),
            pltpu.VMEM((W, W), F32),
            pltpu.VMEM((64, KV), F32),
            pltpu.VMEM((2, Y, 2, 64, KV), BF16),
            pltpu.VMEM((Y, 2, 64, KV), BF16),
            pltpu.VMEM((Y, 2, 64, KV), BF16),
            pltpu.VMEM((Y - 1, 2, 64, KV), BF16),
            pltpu.VMEM((2, 64, KV), BF16),
            pltpu.VMEM((64, KV), BF16),
            dma((5,)),
            dma((NC,)),
            dma((NC,)),
            dma((NC,)),
            dma((NC,)),
            dma((NC,)),
            dma((NC,)),
            dma((NC,)),
            dma((NC,)),
            dma((NC,)),
            dma((3,)),
            dma((3,)),
        ],
        compiler_params=pltpu.CompilerParams(
            collective_id=0, has_side_effects=True, vmem_limit_bytes=60 * 1024 * 1024
        ),
    )(
        inputs.reshape(NC, T, W),
        cotangent.reshape(ROWS, KV),
        norm_gain,
        value_weight[0],
        output_weight[0],
        left_old[0, 0],
        right_old[0],
    )
    return out.reshape(1, 8, 128, W), left[None, None], right[None]


def solution(mesh):
    placed = (
        P(None, None, "dp"),
        P("section", None, None, None),
        P("section", "dp"),
        P("section", "dp", None),
        P("section", None, "dp"),
        P("section", "dp", None, None),
        P("section", "dp", None),
    )
    return jax.shard_map(
        on_device,
        mesh=mesh,
        in_specs=placed,
        out_specs=(
            P("section", None, None, "dp"),
            P("section", "dp", None, None),
            P("section", "dp", None),
        ),
        check_vma=False,
    )
```

time: 778 us -> 272 us (0.35); the launches traced: 767 us -> 271 us
  waiting for transfers between devices: 412 us -> 0 us
  Pallas kernels: 0 us -> 265 us
  starting transfers between devices: 139 us -> 0 us
  matrix products: 136 us -> 0 us
  other arithmetic: 46.8 us -> 0 us
  local copies, waits for them, and re-layouts: 31.9 us -> 5.96 us
    all_to_all x31 -> x0, waiting for transfers between devices: 339 us -> none  [the longest x15 173 us: sent_and_summed(): lax.all_to_all(tiles, axis, split_axis=0, concat_axis=0, tiled=True)]
    pallas_call x0 -> x1, Pallas kernels: none -> 265 us  [on_device(): pl.pallas_call(kernel, out_shape=(jax.ShapeDtypeStruct((NC, T, W), BF16),...]
    dot_general x47 -> x0, matrix products: 136 us -> none  [the longest x15 70.9 us: run_tick(): lax.dot_general(scaled_in, weighted, contract_rows, preferred_element_typ...]
    all_to_all x31 -> x0, starting transfers between devices: 120 us -> none  [the longest x15 61.8 us: sent_and_summed(): lax.all_to_all(tiles, axis, split_axis=0, concat_axis=0, tiled=True)]
    ppermute x15 -> x0, waiting for transfers between devices: 73.3 us -> none  [passed_along(): lax.ppermute(value, axis, [(source, source + steps) for source in range(i...]
    ppermute x15 -> x0, starting transfers between devices: 19.2 us -> none  [passed_along(): lax.ppermute(value, axis, [(source, source + steps) for source in range(i...]
    reduce_sum x31 -> x0, other arithmetic: 17.8 us -> none  [the longest x15 16.9 us: apply_layer(): squares = jnp.sum(floats * floats, axis=1)]
    dynamic_slice x15 -> x0, local copies, waits for them, and re-layouts: 14.6 us -> none  [store_slot(): before = lax.dynamic_index_in_dim(buffer, position, 0, keepdims=False)]
  transfers between devices with their start and end apart: 46 -> 0, of which waited for: 46 -> 0; matrix products, arithmetic and copies ran while one was open for 12% -> 0% of each run, Pallas kernels for 0% -> 0%
where the time goes in v1:
time: 272 us; the launch traced here: 271 us
  Pallas kernels  265 us (97%)
  local copies, waits for them, and re-layouts  5.96 us (2%)
    pallas_call x1, Pallas kernels, on_device(): pl.pallas_call(kernel, out_shape=(jax.ShapeDtypeStruct((NC, T, W), BF16),...  265 us
    unnamed x7, local copies, waits for them, and re-layouts  5.96 us

profile of v1, /device:TPU:70, one launch (start us, length us, event | category | flops | bytes accessed | tf_op | source)
XLA Modules:
  0.0 271.4 jit_solution(2756978008703634867)
XLA Ops:
  0.6 264.8 %shard_map.94 = (bf16[16,64,1024]{2,1,0:T(8,128)(2,1)}, f32[1024,1024]{1,0:T(8,128)}, f32[64,1024]{1,0:T(8,128)}) custom-call(bf16[16,64,1024]{2,1,0:T(8,128)(2,1)} %bitcast.12, bf16[1024,1024]{1,0:T(8,128)(2,1)} %bitcast.13, bf16[1,1024]{1,0:T(2,128)(2,1)} %gain_ref.1, bf16[1024,1024]{1,0:T(8,128)(2,1)} %bitcast.14, bf16[1024,1024]{1,0:T(8,128)(2,1)} %bitcast.15, ...), custom_call_target="tpu_custom_call" | custom-call | tf_op jit(solution)/shard_map/pallas_call | solution.py:265
  265.4 0.0 copy-start
  265.4 3.2 %copy.13 = bf16[1,8,128,1024]{3,2,1,0:T(8,128)(2,1)} copy(bf16[1,8,128,1024]{3,2,1,0:T(8,128)(2,1)} %bitcast.11) | data formatting | bytes 4194304
  268.7 0.0 copy-done
  268.7 0.0 copy-start.1
  268.7 2.0 copy.14
  270.7 0.0 copy-done.1
  270.7 0.7 copy.15
Async XLA Ops:
  265.4 3.2 %copy-start = (f32[1024,1024]{1,0:T(8,128)S(1)}, f32[1024,1024]{1,0:T(8,128)}, u32[]{:S(2)}) copy-start(f32[1024,1024]{1,0:T(8,128)} %get-tuple-element.7) | copy-start | bytes 12582916
  268.7 2.0 copy-start.1

commit v2 on v1

v2 whole, which is shorter than its diff:
```python
import jax
import jax.numpy as jnp
from jax import lax
from jax.experimental import pallas as pl
from jax.experimental.pallas import tpu as pltpu
from jax.sharding import PartitionSpec as P

MESH = pl.DeviceIdType.MESH
F32 = jnp.float32
BF16 = jnp.bfloat16

D = 16384
W = 1024
KV = 1024
ROWS = 1024
T = 32
NC = ROWS // 2 // T
Y = 4
OWN = T // Y
EXT = KV + 128
LAG2, LAG3, LAG4 = 1, 1, 2
ORDER = (1, 2, 3, 4)


def with_pair(rows, scalar):
    high = scalar.astype(BF16).astype(F32)
    low = scalar - high
    lane = lax.broadcasted_iota(jnp.int32, (rows.shape[0], 128), 1)
    pair = jnp.where(lane < 64, high, low)
    return jnp.concatenate([rows, pair], axis=1)


def pair_of(ext):
    return ext[:, KV : KV + 1] + ext[:, KV + 64 : KV + 65]


def kernel(
    x_hbm, cot_hbm, gain_ref, wv_hbm, wo_hbm, left_old_hbm, right_old_hbm,
    out_hbm, left_hbm, right_hbm,
    wv, wo, gain, cot, xbuf, sc, sct, outbuf, part, rs, zs, zr, val, wgt, gb, left, right,
    rpa, rpb, r1a, r1b, r2a, r2b, ta, tb, r3a, r3b,
    load_sem, x_sem, rs_sem, z_sem, ag_sem, out_sem, give_sem, send_sem, r_sem, rsend_sem,
):
    s = lax.axis_index("section")
    d = lax.axis_index("dp")
    zl = d // 8
    core = lax.rem(d, 2)
    y = lax.rem(d, 8) // 2
    zpeer = (s, lax.rem(d + 8, 16))
    cpeer = (s, d + 1 - 2 * core)

    def y_peer(offset):
        return (s, zl * 8 + lax.rem(y + offset, Y) * 2 + core)

    def rows_of(c):
        return pl.ds(pl.multiple_of(core * (ROWS // 2) + c * T, T), T)

    def remote(src, dst, send, recv, device):
        return pltpu.make_async_remote_copy(
            src_ref=src, dst_ref=dst, send_sem=send, recv_sem=recv, device_id=device, device_id_type=MESH
        )

    def wait_for(ref, sem):
        pltpu.make_async_copy(ref, ref, sem).wait()

    @pl.when(s == 0)
    def _():
        def body(c, carry):
            pltpu.make_async_copy(x_hbm.at[core, c], xbuf.at[c, core], x_sem.at[c]).start()
            return carry

        lax.fori_loop(0, NC, body, 0)

    pltpu.make_async_copy(wv_hbm, wv.at[core], load_sem.at[0]).start()
    pltpu.make_async_copy(wo_hbm, wo.at[core], load_sem.at[1]).start()
    load_cot = pltpu.make_async_copy(cot_hbm.at[core], cot, load_sem.at[2])
    load_left = pltpu.make_async_copy(left_old_hbm, left, load_sem.at[3])
    load_right = pltpu.make_async_copy(right_old_hbm, right, load_sem.at[4])
    pltpu.make_async_copy(gain_ref, gain.at[core], load_sem.at[5]).start()
    load_cot.start()
    load_left.start()
    load_right.start()

    barrier = pltpu.get_barrier_semaphore()
    for offset in range(1, Y):
        pl.semaphore_signal(barrier, inc=1, device_id=y_peer(offset), device_id_type=MESH)
    for peer in (zpeer, cpeer, (lax.rem(s + 1, 8), d), (lax.rem(s + 7, 8), d)):
        pl.semaphore_signal(barrier, inc=1, device_id=peer, device_id_type=MESH)
    pl.semaphore_wait(barrier, Y + 3)

    @pl.when(s == 0)
    def _():
        remote(x_hbm.at[1 - core, 0], xbuf.at[0, core], send_sem.at[0], x_sem.at[0], cpeer).start()

    remote(gain_ref, gain.at[core], send_sem.at[1], load_sem.at[5], cpeer).start()
    remote(wv_hbm, wv.at[core], send_sem.at[2], load_sem.at[0], cpeer).start()

    @pl.when(s == 0)
    def _():
        def body(c, carry):
            remote(x_hbm.at[1 - core, c], xbuf.at[c, core], send_sem.at[0], x_sem.at[c], cpeer).start()
            return carry

        lax.fori_loop(1, NC, body, 0)

    remote(wo_hbm, wo.at[core], send_sem.at[3], load_sem.at[1], cpeer).start()
    wait_for(gain, load_sem.at[5])
    wait_for(wv, load_sem.at[0])

    def rs_copy(c, offset):
        return remote(
            part.at[c, lax.rem(y + offset, Y)], rs.at[c, offset - 1], send_sem.at[4], rs_sem.at[c], y_peer(offset)
        )

    def ag_copy(c, offset):
        return remote(val.at[c, y], val.at[c, y], send_sem.at[5], ag_sem.at[c], y_peer(offset))

    def stage1(c):
        wait_for(xbuf.at[c], x_sem.at[c])
        product = None
        squares = None
        scaled = []
        for h in range(2):
            floats = xbuf[c, h].astype(F32)
            scaled.append((floats * gain[h].astype(F32)).astype(BF16))
            sums = jnp.sum(floats * floats, axis=1, keepdims=True)
            squares = sums if h == 0 else squares + sums
            dot = jnp.dot(scaled[h], wv[h], preferred_element_type=F32)
            product = dot if h == 0 else product + dot
        both = with_pair(product, squares)
        part[c] = both.reshape(Y, OWN, EXT).astype(BF16)
        for offset in range(1, Y):
            rs_copy(c, offset).start()
        sc[rows_of(c), :] = jnp.where(core == 0, scaled[0], scaled[1])
        sct[c] = jnp.where(core == 0, scaled[1], scaled[0])
        remote(sct.at[c], sc.at[rows_of(c)], send_sem.at[6], give_sem.at[0], cpeer).start()

    def stage2(c):
        wait_for(rs.at[c], rs_sem.at[c])
        total = part[c, y].astype(F32)
        for j in range(Y - 1):
            total += rs[c, j].astype(F32)
        zs[c] = with_pair(total[:, :KV], pair_of(total)).astype(BF16)
        remote(zs.at[c], zr.at[c], send_sem.at[7], z_sem.at[c], zpeer).start()

    def stage3(c):
        wait_for(zr.at[c], z_sem.at[c])
        total = zs[c].astype(F32) + zr[c].astype(F32)
        inv = lax.rsqrt(pair_of(total) / D + 0.25)
        val[c, y] = with_pair(inv * total[:, :KV], inv).astype(BF16)
        for offset in range(1, Y):
            ag_copy(c, offset).start()

    def stage4(c):
        wait_for(rs.at[c], ag_sem.at[c])
        both = val[c].astype(F32).reshape(T, EXT)
        values = both[:, :KV].astype(BF16)
        for h in range(2):
            result = xbuf[c, h].astype(F32) + jnp.dot(values, wo[h], preferred_element_type=F32)
            outbuf[c, h] = result.astype(BF16)

        @pl.when(s < 7)
        def _():
            remote(outbuf.at[c], xbuf.at[c], send_sem.at[8], x_sem.at[c], (s + 1, d)).start()

        wgt[rows_of(c), :] = (pair_of(both) * cot[c].astype(F32)).astype(BF16)
        remote(wgt.at[rows_of(c)], wgt.at[rows_of(c)], send_sem.at[9], give_sem.at[1], cpeer).start()
        pltpu.make_async_copy(outbuf.at[c, core], out_hbm.at[core, c], out_sem.at[0]).start()
        remote(outbuf.at[c, 1 - core], out_hbm.at[core, c], send_sem.at[10], out_sem.at[1], cpeer).start()

    stages = {1: (stage1, 0), 2: (stage2, LAG2), 3: (stage3, LAG3), 4: (stage4, LAG4)}

    def tick(k, carry):
        @pl.when(k == LAG4)
        def _():
            wait_for(wo, load_sem.at[1])
            load_cot.wait()

        for which in ORDER:
            stage, lag = stages[which]

            @pl.when((k >= lag) & (k < NC + lag))
            def _(stage=stage, lag=lag):
                stage(k - lag)

        return carry

    lax.fori_loop(0, NC + LAG4, tick, 0)

    over_rows = (((0,), (0,)), ((), ()))
    over_cols = (((1,), (1,)), ((), ()))
    STEP = 256

    def block(i):
        return pl.ds(pl.multiple_of(i * STEP, STEP), STEP)

    other = pl.ds(pl.multiple_of((1 - core) * (ROWS // 2), ROWS // 2), ROWS // 2)
    wait_for(sc.at[other], give_sem.at[0])
    wait_for(wgt.at[other], give_sem.at[1])

    def grad_block(i, carry):
        gb[block(i), :] = lax.dot_general(
            sc[:, block(i)], wgt[...], over_rows, preferred_element_type=F32
        ).astype(BF16)
        return carry

    lax.fori_loop(0, W // STEP, grad_block, 0)

    half = KV // 2

    def right_rows(i, h):
        return lax.dot_general(
            gb[:, block(i)], gb[:, h * half : (h + 1) * half], over_rows, preferred_element_type=F32
        ).astype(BF16)

    def right_b(i, carry):
        rows = right_rows(i, 1)
        for j in range(4):
            rpb[j % 2, i // 2, 2 * lax.rem(i, 2) + j // 2] = rows[64 * j : 64 * (j + 1), :]
        return carry

    def right_a(i, carry):
        rows = right_rows(i, 0)
        for j in range(4):
            rpa[j % 2, 2 * lax.rem(i, 2) + j // 2, i // 2] = rows[64 * j : 64 * (j + 1), :]
        return carry

    core_b = remote(rpb.at[1 - core], r1b, rsend_sem.at[0], r_sem.at[0], cpeer)
    core_a = remote(rpa.at[1 - core], r1a, rsend_sem.at[1], r_sem.at[1], cpeer)
    lax.fori_loop(0, KV // STEP, right_b, 0)
    core_b.start()
    lax.fori_loop(0, KV // STEP, right_a, 0)
    core_a.start()

    def left_block(i, carry):
        add = lax.dot_general(gb[block(i), :], gb[...], over_cols, preferred_element_type=F32)
        left[block(i), :] = left[block(i), :] + add * (1.0 / 1024)
        return carry

    core_b.wait()
    r1b[...] = (rpb[core].astype(F32) + r1b[...].astype(F32)).astype(BF16)
    z_b = remote(r1b.at[1 - zl], r2b, rsend_sem.at[2], r_sem.at[2], zpeer)
    z_b.start()
    core_a.wait()
    r1a[...] = (rpa[core].astype(F32) + r1a[...].astype(F32)).astype(BF16)
    for offset in range(1, Y):
        remote(
            r1a.at[lax.rem(y + offset, Y)], r2a.at[offset - 1], rsend_sem.at[3], r_sem.at[3], y_peer(offset)
        ).start()
    load_left.wait()
    load_right.wait()
    lax.fori_loop(0, W // STEP, left_block, 0)
    left_copy = pltpu.make_async_copy(left, left_hbm, load_sem.at[3])
    left_copy.start()
    z_b.wait()
    tb[...] = (r1b[zl].astype(F32) + r2b[...].astype(F32)).astype(BF16)
    for offset in range(1, Y):
        remote(
            tb.at[lax.rem(y + offset, Y)], r3b.at[offset - 1], rsend_sem.at[4], r_sem.at[4], y_peer(offset)
        ).start()
    wait_for(r2a, r_sem.at[3])
    summed = r1a[y].astype(F32)
    for j in range(Y - 1):
        summed += r2a[j].astype(F32)
    ta[...] = summed.astype(BF16)
    z_a = remote(ta.at[1 - zl], r3a, rsend_sem.at[5], r_sem.at[5], zpeer)
    z_a.start()
    wait_for(r3b, r_sem.at[4])
    summed = tb[y].astype(F32)
    for j in range(Y - 1):
        summed += r3b[j].astype(F32)
    right[:, half:] = right[:, half:] + summed * (1.0 / D)
    z_a.wait()
    right[:, :half] = right[:, :half] + (ta[zl].astype(F32) + r3a[...].astype(F32)) * (1.0 / D)
    right_copy = pltpu.make_async_copy(right, right_hbm, load_sem.at[4])
    right_copy.start()

    wait_for(r2a, rsend_sem.at[3])
    wait_for(r3b, rsend_sem.at[4])
    wait_for(gain.at[0], send_sem.at[1])
    wait_for(wv.at[0], send_sem.at[2])
    wait_for(wo.at[0], send_sem.at[3])
    wait_for(rs, send_sem.at[4])
    wait_for(rs, send_sem.at[5])
    wait_for(sct, send_sem.at[6])
    wait_for(zs, send_sem.at[7])
    wait_for(wgt.at[other], send_sem.at[9])
    wait_for(sct, send_sem.at[10])
    wait_for(sct, out_sem.at[0])
    wait_for(sct, out_sem.at[1])

    @pl.when(s == 0)
    def _():
        wait_for(sct, send_sem.at[0])

    @pl.when(s < 7)
    def _():
        wait_for(outbuf, send_sem.at[8])

    left_copy.wait()
    right_copy.wait()


def on_device(inputs, cotangent, norm_gain, value_weight, output_weight, left_old, right_old):
    any_space = pl.BlockSpec(memory_space=pl.ANY)
    dma = pltpu.SemaphoreType.DMA
    out, left, right = pl.pallas_call(
        kernel,
        out_shape=(
            jax.ShapeDtypeStruct((2, NC, T, W), BF16),
            jax.ShapeDtypeStruct((W, W), F32),
            jax.ShapeDtypeStruct((64, KV), F32),
        ),
        in_specs=[any_space] * 7,
        out_specs=(any_space, any_space, any_space),
        scratch_shapes=[
            pltpu.VMEM((2, W, KV), BF16),
            pltpu.VMEM((2, KV, W), BF16),
            pltpu.VMEM((2, 1, W), BF16),
            pltpu.VMEM((NC, T, KV), BF16),
            pltpu.VMEM((NC, 2, T, W), BF16),
            pltpu.VMEM((ROWS, W), BF16),
            pltpu.VMEM((NC, T, W), BF16),
            pltpu.VMEM((NC, 2, T, W), BF16),
            pltpu.VMEM((NC, Y, OWN, EXT), BF16),
            pltpu.VMEM((NC, Y - 1, OWN, EXT), BF16),
            pltpu.VMEM((NC, OWN, EXT), BF16),
            pltpu.VMEM((NC, OWN, EXT), BF16),
            pltpu.VMEM((NC, Y, OWN, EXT), BF16),
            pltpu.VMEM((ROWS, KV), BF16),
            pltpu.VMEM((W, KV), BF16),
            pltpu.VMEM((W, W), F32),
            pltpu.VMEM((64, KV), F32),
            pltpu.VMEM((2, Y, 2, 64, KV // 2), BF16),
            pltpu.VMEM((2, 2, Y, 64, KV // 2), BF16),
            pltpu.VMEM((Y, 2, 64, KV // 2), BF16),
            pltpu.VMEM((2, Y, 64, KV // 2), BF16),
            pltpu.VMEM((Y - 1, 2, 64, KV // 2), BF16),
            pltpu.VMEM((Y, 64, KV // 2), BF16),
            pltpu.VMEM((2, 64, KV // 2), BF16),
            pltpu.VMEM((Y, 64, KV // 2), BF16),
            pltpu.VMEM((64, KV // 2), BF16),
            pltpu.VMEM((Y - 1, 64, KV // 2), BF16),
            dma((6,)),
            dma((NC,)),
            dma((NC,)),
            dma((NC,)),
            dma((NC,)),
            dma((2,)),
            dma((2,)),
            dma((11,)),
            dma((6,)),
            dma((6,)),
        ],
        compiler_params=pltpu.CompilerParams(
            collective_id=0, has_side_effects=True, vmem_limit_bytes=60 * 1024 * 1024
        ),
    )(
        inputs.reshape(2, NC, T, W),
        cotangent.reshape(2, NC, T, KV),
        norm_gain,
        value_weight[0],
        output_weight[0],
        left_old[0, 0],
        right_old[0],
    )
    return out.reshape(1, 8, 128, W), left[None, None], right[None]


def solution(mesh):
    placed = (
        P(None, None, "dp"),
        P("section", None, None, None),
        P("section", "dp"),
        P("section", "dp", None),
        P("section", None, "dp"),
        P("section", "dp", None, None),
        P("section", "dp", None),
    )
    return jax.shard_map(
        on_device,
        mesh=mesh,
        in_specs=placed,
        out_specs=(
            P("section", None, None, "dp"),
            P("section", "dp", None, None),
            P("section", "dp", None),
        ),
        check_vma=False,
    )
```

time: 272 us -> 293 us (1.077)
  Pallas kernels: 265 us -> 287 us
    pallas_call x1, Pallas kernels: 265 us -> 287 us  [on_device(): pl.pallas_call(kernel, out_shape=(jax.ShapeDtypeStruct((2, NC, T, W), BF1...]
where the time goes in v2:
time: 293 us
  Pallas kernels  287 us (98%)
  local copies, waits for them, and re-layouts  5.96 us (2%)
    pallas_call x1, Pallas kernels, on_device(): pl.pallas_call(kernel, out_shape=(jax.ShapeDtypeStruct((2, NC, T, W), BF1...  287 us
    unnamed x7, local copies, waits for them, and re-layouts  5.96 us

profile of v2, /device:TPU:70, one launch (start us, length us, event | category | flops | bytes accessed | tf_op | source)
XLA Modules:
  0.0 293.2 jit_solution(4246612892529951107)
XLA Ops:
  0.6 286.6 %shard_map.94 = (bf16[2,16,32,1024]{3,2,1,0:T(8,128)(2,1)}, f32[1024,1024]{1,0:T(8,128)}, f32[64,1024]{1,0:T(8,128)}) custom-call(bf16[2,16,32,1024]{3,2,1,0:T(8,128)(2,1)} %bitcast.12, bf16[2,16,32,1024]{3,2,1,0:T(8,128)(2,1)} %bitcast.13, bf16[1,1024]{1,0:T(2,128)(2,1)} %gain_ref.1, bf16[1024,1024]{1,0:T(8,128)(2,1)} %bitcast.14, ...), custom_call_target="tpu_custom_call" | custom-call | tf_op jit(solution)/shard_map/pallas_call | solution.py:307
  287.3 0.0 copy-start
  287.3 3.2 %copy.13 = bf16[1,8,128,1024]{3,2,1,0:T(8,128)(2,1)} copy(bf16[1,8,128,1024]{3,2,1,0:T(8,128)(2,1)} %bitcast.11) | data formatting | bytes 4194304
  290.5 0.0 copy-done
  290.5 0.0 copy-start.1
  290.5 2.0 copy.14
  292.5 0.0 copy-done.1
  292.5 0.7 copy.15
Async XLA Ops:
  287.3 3.2 %copy-start = (f32[1024,1024]{1,0:T(8,128)S(1)}, f32[1024,1024]{1,0:T(8,128)}, u32[]{:S(2)}) copy-start(f32[1024,1024]{1,0:T(8,128)} %get-tuple-element.7) | copy-start | bytes 12582916
  290.5 2.0 copy-start.1

commit v3 on v2

--- a/solution.py
+++ b/solution.py
@@ -18,8 +18,11 @@
 Y = 4
 OWN = T // Y
 EXT = KV + 128
-LAG2, LAG3, LAG4 = 1, 1, 2
-ORDER = (1, 2, 3, 4)
+LAG2, LAG3, LAG4 = 1, 2, 3
+ORDER = (0, 1, 2, 3, 4)
+LAG0 = -1
+LATE = 4
+PIECES = 4
 
 
 def with_pair(rows, scalar):
@@ -37,15 +40,16 @@
 def kernel(
     x_hbm, cot_hbm, gain_ref, wv_hbm, wo_hbm, left_old_hbm, right_old_hbm,
     out_hbm, left_hbm, right_hbm,
-    wv, wo, gain, cot, xbuf, sc, sct, outbuf, part, rs, zs, zr, val, wgt, gb, left, right,
+    wv, wo, wop, gain, cot, xbuf, vin, sc, sct, outbuf, part, rs, zs, zr, val, wgt, gb, left, right,
     rpa, rpb, r1a, r1b, r2a, r2b, ta, tb, r3a, r3b,
-    load_sem, x_sem, rs_sem, z_sem, ag_sem, out_sem, give_sem, send_sem, r_sem, rsend_sem,
+    load_sem, x_sem, rs_sem, z_sem, ag_sem, out_sem, give_sem, v_sem, v2_sem, pre_sem, send_sem, r_sem, rsend_sem,
 ):
     s = lax.axis_index("section")
     d = lax.axis_index("dp")
     zl = d // 8
     core = lax.rem(d, 2)
     y = lax.rem(d, 8) // 2
+    odd = lax.rem(s, 2) == 1
     zpeer = (s, lax.rem(d + 8, 16))
     cpeer = (s, d + 1 - 2 * core)
 
@@ -84,9 +88,13 @@
     barrier = pltpu.get_barrier_semaphore()
     for offset in range(1, Y):
         pl.semaphore_signal(barrier, inc=1, device_id=y_peer(offset), device_id_type=MESH)
-    for peer in (zpeer, cpeer, (lax.rem(s + 1, 8), d), (lax.rem(s + 7, 8), d)):
+    for step in (1, 7):
+        for offset in range(Y):
+            peer = (lax.rem(s + step, 8), y_peer(offset)[1])
+            pl.semaphore_signal(barrier, inc=1, device_id=peer, device_id_type=MESH)
+    for peer in (zpeer, cpeer, (lax.rem(s + 2, 8), d), (lax.rem(s + 6, 8), d)):
         pl.semaphore_signal(barrier, inc=1, device_id=peer, device_id_type=MESH)
-    pl.semaphore_wait(barrier, Y + 3)
+    pl.semaphore_wait(barrier, Y - 1 + 2 * Y + 4)
 
     @pl.when(s == 0)
     def _():
@@ -104,6 +112,25 @@
         lax.fori_loop(1, NC, body, 0)
 
     remote(wo_hbm, wo.at[core], send_sem.at[3], load_sem.at[1], cpeer).start()
+
+    def piece(i):
+        return pl.ds(i * (KV // PIECES), KV // PIECES)
+
+    @pl.when((s >= LATE - 1) & (s < 7))
+    def _():
+        for i in range(PIECES):
+            remote(
+                wo_hbm.at[piece(i)], wop.at[core, piece(i)], send_sem.at[11], pre_sem.at[i], (s + 1, d)
+            ).start()
+
+    @pl.when(s >= LATE)
+    def _():
+        for i in range(PIECES):
+            ours = wop.at[core, piece(i)]
+            wait_for(ours, pre_sem.at[i])
+            remote(ours, ours, send_sem.at[12], pre_sem.at[PIECES], cpeer).start()
+        wait_for(wop.at[0], pre_sem.at[PIECES])
+
     wait_for(gain, load_sem.at[5])
     wait_for(wv, load_sem.at[0])
 
@@ -115,8 +142,31 @@
     def ag_copy(c, offset):
         return remote(val.at[c, y], val.at[c, y], send_sem.at[5], ag_sem.at[c], y_peer(offset))
 
+    def stage0(c):
+        @pl.when((s >= LATE) & jnp.logical_not(odd))
+        def _():
+            wait_for(vin.at[c, y], v_sem.at[c])
+            for offset in range(1, Y):
+                remote(vin.at[c, y], vin.at[c, y], send_sem.at[15], v2_sem.at[c], y_peer(offset)).start()
+
     def stage1(c):
         wait_for(xbuf.at[c], x_sem.at[c])
+
+        @pl.when(s >= LATE)
+        def _():
+            @pl.when(odd)
+            def _():
+                wait_for(vin.at[c], v_sem.at[c])
+
+            @pl.when(jnp.logical_not(odd))
+            def _():
+                wait_for(rs.at[c], v2_sem.at[c])
+
+            before = vin[c].astype(F32).reshape(T, EXT)[:, :KV].astype(BF16)
+            for h in range(2):
+                made = xbuf[c, h].astype(F32) + jnp.dot(before, wop[h], preferred_element_type=F32)
+                xbuf[c, h] = made.astype(BF16)
+
         product = None
         squares = None
         scaled = []
@@ -148,6 +198,18 @@
         total = zs[c].astype(F32) + zr[c].astype(F32)
         inv = lax.rsqrt(pair_of(total) / D + 0.25)
         val[c, y] = with_pair(inv * total[:, :KV], inv).astype(BF16)
+
+        @pl.when((s >= LATE - 1) & (s < 7))
+        def _():
+            remote(val.at[c, y], vin.at[c, y], send_sem.at[13], v_sem.at[c], (s + 1, d)).start()
+
+            @pl.when(jnp.logical_not(odd))
+            def _():
+                for offset in range(1, Y):
+                    remote(
+                        val.at[c, y], vin.at[c, y], send_sem.at[15], v_sem.at[c], (s + 1, y_peer(offset)[1])
+                    ).start()
+
         for offset in range(1, Y):
             ag_copy(c, offset).start()
 
@@ -159,16 +221,24 @@
             result = xbuf[c, h].astype(F32) + jnp.dot(values, wo[h], preferred_element_type=F32)
             outbuf[c, h] = result.astype(BF16)
 
-        @pl.when(s < 7)
+        @pl.when(s < LATE - 1)
         def _():
             remote(outbuf.at[c], xbuf.at[c], send_sem.at[8], x_sem.at[c], (s + 1, d)).start()
+
+        @pl.when((s >= LATE - 2) & (s < 6))
+        def _():
+            remote(outbuf.at[c], xbuf.at[c], send_sem.at[14], x_sem.at[c], (s + 2, d)).start()
 
         wgt[rows_of(c), :] = (pair_of(both) * cot[c].astype(F32)).astype(BF16)
         remote(wgt.at[rows_of(c)], wgt.at[rows_of(c)], send_sem.at[9], give_sem.at[1], cpeer).start()
         pltpu.make_async_copy(outbuf.at[c, core], out_hbm.at[core, c], out_sem.at[0]).start()
         remote(outbuf.at[c, 1 - core], out_hbm.at[core, c], send_sem.at[10], out_sem.at[1], cpeer).start()
 
-    stages = {1: (stage1, 0), 2: (stage2, LAG2), 3: (stage3, LAG3), 4: (stage4, LAG4)}
+    stages = {0: (stage0, LAG0), 1: (stage1, 0), 2: (stage2, LAG2), 3: (stage3, LAG3), 4: (stage4, LAG4)}
+
+    stage0(0)
+    if LAG0 == -2:
+        stage0(1)
 
     def tick(k, carry):
         @pl.when(k == LAG4)
@@ -293,9 +363,27 @@
     def _():
         wait_for(sct, send_sem.at[0])
 
-    @pl.when(s < 7)
+    @pl.when(s < LATE - 1)
     def _():
         wait_for(outbuf, send_sem.at[8])
+
+    @pl.when((s >= LATE - 2) & (s < 6))
+    def _():
+        wait_for(outbuf, send_sem.at[14])
+
+    @pl.when((s >= LATE - 1) & (s < 7))
+    def _():
+        wait_for(wo.at[0], send_sem.at[11])
+        wait_for(zs, send_sem.at[13])
+
+    @pl.when(s >= LATE)
+    def _():
+        wait_for(wop.at[0], send_sem.at[12])
+
+    @pl.when((s >= LATE) & (s < 7) & jnp.logical_not(odd))
+    def _():
+        wait_for(rs, send_sem.at[15])
+        wait_for(rs, send_sem.at[15])
 
     left_copy.wait()
     right_copy.wait()
@@ -316,9 +404,11 @@
         scratch_shapes=[
             pltpu.VMEM((2, W, KV), BF16),
             pltpu.VMEM((2, KV, W), BF16),
+            pltpu.VMEM((2, KV, W), BF16),
             pltpu.VMEM((2, 1, W), BF16),
             pltpu.VMEM((NC, T, KV), BF16),
             pltpu.VMEM((NC, 2, T, W), BF16),
+            pltpu.VMEM((NC, Y, OWN, EXT), BF16),
             pltpu.VMEM((ROWS, W), BF16),
             pltpu.VMEM((NC, T, W), BF16),
             pltpu.VMEM((NC, 2, T, W), BF16),
@@ -348,7 +438,10 @@
             dma((NC,)),
             dma((2,)),
             dma((2,)),
-            dma((11,)),
+            dma((NC,)),
+            dma((NC,)),
+            dma((PIECES + 1,)),
+            dma((16,)),
             dma((6,)),
             dma((6,)),
         ],

time: 293 us -> 239 us (0.82)
  Pallas kernels: 287 us -> 232 us
    pallas_call x1, Pallas kernels: 287 us -> 232 us  [on_device(): pl.pallas_call(kernel, out_shape=(jax.ShapeDtypeStruct((2, NC, T, W), BF1...]
where the time goes in v3:
time: 239 us
  Pallas kernels  232 us (97%)
  local copies, waits for them, and re-layouts  5.96 us (2%)
    pallas_call x1, Pallas kernels, on_device(): pl.pallas_call(kernel, out_shape=(jax.ShapeDtypeStruct((2, NC, T, W), BF1...  232 us
    unnamed x7, local copies, waits for them, and re-layouts  5.96 us

profile of v3, /device:TPU:70, one launch (start us, length us, event | category | flops | bytes accessed | tf_op | source)
XLA Modules:
  0.0 239.0 jit_solution(10155494324003630318)
XLA Ops:
  0.6 232.4 %shard_map.94 = (bf16[2,16,32,1024]{3,2,1,0:T(8,128)(2,1)}, f32[1024,1024]{1,0:T(8,128)}, f32[64,1024]{1,0:T(8,128)}) custom-call(bf16[2,16,32,1024]{3,2,1,0:T(8,128)(2,1)} %bitcast.12, bf16[2,16,32,1024]{3,2,1,0:T(8,128)(2,1)} %bitcast.13, bf16[1,1024]{1,0:T(2,128)(2,1)} %gain_ref.1, bf16[1024,1024]{1,0:T(8,128)(2,1)} %bitcast.14, ...), custom_call_target="tpu_custom_call" | custom-call | tf_op jit(solution)/shard_map/pallas_call | solution.py:395
  233.1 0.0 copy-start
  233.1 3.2 %copy.13 = bf16[1,8,128,1024]{3,2,1,0:T(8,128)(2,1)} copy(bf16[1,8,128,1024]{3,2,1,0:T(8,128)(2,1)} %bitcast.11) | data formatting | bytes 4194304
  236.3 0.0 copy-done
  236.3 0.0 copy-start.1
  236.3 2.0 copy.14
  238.3 0.0 copy-done.1
  238.3 0.7 copy.15
Async XLA Ops:
  233.1 3.2 %copy-start = (f32[1024,1024]{1,0:T(8,128)S(1)}, f32[1024,1024]{1,0:T(8,128)}, u32[]{:S(2)}) copy-start(f32[1024,1024]{1,0:T(8,128)} %get-tuple-element.7) | copy-start | bytes 12582916
  236.3 2.0 copy-start.1

commit v4 on v3

--- a/solution.py
+++ b/solution.py
@@ -160,9 +160,9 @@
 
             @pl.when(jnp.logical_not(odd))
             def _():
-                wait_for(rs.at[c], v2_sem.at[c])
-
-            before = vin[c].astype(F32).reshape(T, EXT)[:, :KV].astype(BF16)
+                wait_for(vin.at[c, pl.ds(0, Y - 1)], v2_sem.at[c])
+
+            before = vin[c].astype(F32).reshape(T, KV).astype(BF16)
             for h in range(2):
                 made = xbuf[c, h].astype(F32) + jnp.dot(before, wop[h], preferred_element_type=F32)
                 xbuf[c, h] = made.astype(BF16)
@@ -201,13 +201,13 @@
 
         @pl.when((s >= LATE - 1) & (s < 7))
         def _():
-            remote(val.at[c, y], vin.at[c, y], send_sem.at[13], v_sem.at[c], (s + 1, d)).start()
+            remote(val.at[c, y, :, pl.ds(0, KV)], vin.at[c, y], send_sem.at[13], v_sem.at[c], (s + 1, d)).start()
 
             @pl.when(jnp.logical_not(odd))
             def _():
                 for offset in range(1, Y):
                     remote(
-                        val.at[c, y], vin.at[c, y], send_sem.at[15], v_sem.at[c], (s + 1, y_peer(offset)[1])
+                        val.at[c, y, :, pl.ds(0, KV)], vin.at[c, y], send_sem.at[15], v_sem.at[c], (s + 1, y_peer(offset)[1])
                     ).start()
 
         for offset in range(1, Y):
@@ -234,7 +234,8 @@
         pltpu.make_async_copy(outbuf.at[c, core], out_hbm.at[core, c], out_sem.at[0]).start()
         remote(outbuf.at[c, 1 - core], out_hbm.at[core, c], send_sem.at[10], out_sem.at[1], cpeer).start()
 
-    stages = {0: (stage0, LAG0), 1: (stage1, 0), 2: (stage2, LAG2), 3: (stage3, LAG3), 4: (stage4, LAG4)}
+    lag4 = jnp.where(s >= LATE - 1, 4, LAG4)
+    stages = {0: (stage0, LAG0), 1: (stage1, 0), 2: (stage2, LAG2), 3: (stage3, LAG3), 4: (stage4, lag4)}
 
     stage0(0)
     if LAG0 == -2:
@@ -255,7 +256,7 @@
 
         return carry
 
-    lax.fori_loop(0, NC + LAG4, tick, 0)
+    lax.fori_loop(0, NC + 4, tick, 0)
 
     over_rows = (((0,), (0,)), ((), ()))
     over_cols = (((1,), (1,)), ((), ()))
@@ -374,7 +375,7 @@
     @pl.when((s >= LATE - 1) & (s < 7))
     def _():
         wait_for(wo.at[0], send_sem.at[11])
-        wait_for(zs, send_sem.at[13])
+        wait_for(vin.at[:, 0], send_sem.at[13])
 
     @pl.when(s >= LATE)
     def _():
@@ -382,8 +383,8 @@
 
     @pl.when((s >= LATE) & (s < 7) & jnp.logical_not(odd))
     def _():
-        wait_for(rs, send_sem.at[15])
-        wait_for(rs, send_sem.at[15])
+        wait_for(vin.at[:, pl.ds(0, Y - 1)], send_sem.at[15])
+        wait_for(vin.at[:, pl.ds(0, Y - 1)], send_sem.at[15])
 
     left_copy.wait()
     right_copy.wait()
@@ -408,7 +409,7 @@
             pltpu.VMEM((2, 1, W), BF16),
             pltpu.VMEM((NC, T, KV), BF16),
             pltpu.VMEM((NC, 2, T, W), BF16),
-            pltpu.VMEM((NC, Y, OWN, EXT), BF16),
+            pltpu.VMEM((NC, Y, OWN, KV), BF16),
             pltpu.VMEM((ROWS, W), BF16),
             pltpu.VMEM((NC, T, W), BF16),
             pltpu.VMEM((NC, 2, T, W), BF16),

time: 239 us -> 235 us (0.983)
  Pallas kernels: 232 us -> 228 us
    pallas_call x1, Pallas kernels: 232 us -> 228 us  [on_device(): pl.pallas_call(kernel, out_shape=(jax.ShapeDtypeStruct((2, NC, T, W), BF1...]
where the time goes in v4:
time: 235 us; the launch traced here: 234 us
  Pallas kernels  228 us (97%)
  local copies, waits for them, and re-layouts  5.96 us (3%)
    pallas_call x1, Pallas kernels, on_device(): pl.pallas_call(kernel, out_shape=(jax.ShapeDtypeStruct((2, NC, T, W), BF1...  228 us
    unnamed x7, local copies, waits for them, and re-layouts  5.96 us

profile of v4, /device:TPU:70, one launch (start us, length us, event | category | flops | bytes accessed | tf_op | source)
XLA Modules:
  0.0 234.5 jit_solution(16742251248624423429)
XLA Ops:
  0.6 227.9 %shard_map.94 = (bf16[2,16,32,1024]{3,2,1,0:T(8,128)(2,1)}, f32[1024,1024]{1,0:T(8,128)}, f32[64,1024]{1,0:T(8,128)}) custom-call(bf16[2,16,32,1024]{3,2,1,0:T(8,128)(2,1)} %bitcast.12, bf16[2,16,32,1024]{3,2,1,0:T(8,128)(2,1)} %bitcast.13, bf16[1,1024]{1,0:T(2,128)(2,1)} %gain_ref.1, bf16[1024,1024]{1,0:T(8,128)(2,1)} %bitcast.14, ...), custom_call_target="tpu_custom_call" | custom-call | tf_op jit(solution)/shard_map/pallas_call | solution.py:396
  228.5 0.0 copy-start
  228.5 3.2 %copy.13 = bf16[1,8,128,1024]{3,2,1,0:T(8,128)(2,1)} copy(bf16[1,8,128,1024]{3,2,1,0:T(8,128)(2,1)} %bitcast.11) | data formatting | bytes 4194304
  231.8 0.0 copy-done
  231.8 0.0 copy-start.1
  231.8 2.0 copy.14
  233.8 0.0 copy-done.1
  233.8 0.7 copy.15
Async XLA Ops:
  228.5 3.2 %copy-start = (f32[1024,1024]{1,0:T(8,128)S(1)}, f32[1024,1024]{1,0:T(8,128)}, u32[]{:S(2)}) copy-start(f32[1024,1024]{1,0:T(8,128)} %get-tuple-element.7) | copy-start | bytes 12582916
  231.8 2.0 copy-start.1

commit v5 on v4

--- a/solution.py
+++ b/solution.py
@@ -19,8 +19,7 @@
 OWN = T // Y
 EXT = KV + 128
 LAG2, LAG3, LAG4 = 1, 2, 3
-ORDER = (0, 1, 2, 3, 4)
-LAG0 = -1
+LAGP = 4
 LATE = 4
 PIECES = 4
 
@@ -42,7 +41,7 @@
     out_hbm, left_hbm, right_hbm,
     wv, wo, wop, gain, cot, xbuf, vin, sc, sct, outbuf, part, rs, zs, zr, val, wgt, gb, left, right,
     rpa, rpb, r1a, r1b, r2a, r2b, ta, tb, r3a, r3b,
-    load_sem, x_sem, rs_sem, z_sem, ag_sem, out_sem, give_sem, v_sem, v2_sem, pre_sem, send_sem, r_sem, rsend_sem,
+    load_sem, x_sem, rs_sem, z_sem, ag_sem, out_sem, give_sem, v_sem, pre_sem, send_sem, r_sem, rsend_sem,
 ):
     s = lax.axis_index("section")
     d = lax.axis_index("dp")
@@ -142,26 +141,12 @@
     def ag_copy(c, offset):
         return remote(val.at[c, y], val.at[c, y], send_sem.at[5], ag_sem.at[c], y_peer(offset))
 
-    def stage0(c):
-        @pl.when((s >= LATE) & jnp.logical_not(odd))
-        def _():
-            wait_for(vin.at[c, y], v_sem.at[c])
-            for offset in range(1, Y):
-                remote(vin.at[c, y], vin.at[c, y], send_sem.at[15], v2_sem.at[c], y_peer(offset)).start()
-
     def stage1(c):
         wait_for(xbuf.at[c], x_sem.at[c])
 
         @pl.when(s >= LATE)
         def _():
-            @pl.when(odd)
-            def _():
-                wait_for(vin.at[c], v_sem.at[c])
-
-            @pl.when(jnp.logical_not(odd))
-            def _():
-                wait_for(vin.at[c, pl.ds(0, Y - 1)], v2_sem.at[c])
-
+            wait_for(vin.at[c], v_sem.at[c])
             before = vin[c].astype(F32).reshape(T, KV).astype(BF16)
             for h in range(2):
                 made = xbuf[c, h].astype(F32) + jnp.dot(before, wop[h], preferred_element_type=F32)
@@ -181,6 +166,11 @@
         part[c] = both.reshape(Y, OWN, EXT).astype(BF16)
         for offset in range(1, Y):
             rs_copy(c, offset).start()
+
+        @pl.when((s >= LATE) & (s < 7) & jnp.logical_not(odd))
+        def _():
+            remote(xbuf.at[c, 1], xbuf.at[c, 1], send_sem.at[15], x_sem.at[c], (s + 1, d)).start()
+
         sc[rows_of(c), :] = jnp.where(core == 0, scaled[0], scaled[1])
         sct[c] = jnp.where(core == 0, scaled[1], scaled[0])
         remote(sct.at[c], sc.at[rows_of(c)], send_sem.at[6], give_sem.at[0], cpeer).start()
@@ -201,14 +191,10 @@
 
         @pl.when((s >= LATE - 1) & (s < 7))
         def _():
-            remote(val.at[c, y, :, pl.ds(0, KV)], vin.at[c, y], send_sem.at[13], v_sem.at[c], (s + 1, d)).start()
-
-            @pl.when(jnp.logical_not(odd))
-            def _():
-                for offset in range(1, Y):
-                    remote(
-                        val.at[c, y, :, pl.ds(0, KV)], vin.at[c, y], send_sem.at[15], v_sem.at[c], (s + 1, y_peer(offset)[1])
-                    ).start()
+            for offset in range(Y):
+                remote(
+                    val.at[c, y, :, pl.ds(0, KV)], vin.at[c, y], send_sem.at[13], v_sem.at[c], (s + 1, y_peer(offset)[1])
+                ).start()
 
         for offset in range(1, Y):
             ag_copy(c, offset).start()
@@ -225,38 +211,41 @@
         def _():
             remote(outbuf.at[c], xbuf.at[c], send_sem.at[8], x_sem.at[c], (s + 1, d)).start()
 
-        @pl.when((s >= LATE - 2) & (s < 6))
+        @pl.when((s >= LATE - 2) & (s < 6) & jnp.logical_not(odd))
         def _():
             remote(outbuf.at[c], xbuf.at[c], send_sem.at[14], x_sem.at[c], (s + 2, d)).start()
+
+        @pl.when((s >= LATE - 2) & (s < 6) & odd)
+        def _():
+            remote(outbuf.at[c, 0], xbuf.at[c, 0], send_sem.at[14], x_sem.at[c], (s + 2, d)).start()
 
         wgt[rows_of(c), :] = (pair_of(both) * cot[c].astype(F32)).astype(BF16)
         remote(wgt.at[rows_of(c)], wgt.at[rows_of(c)], send_sem.at[9], give_sem.at[1], cpeer).start()
         pltpu.make_async_copy(outbuf.at[c, core], out_hbm.at[core, c], out_sem.at[0]).start()
         remote(outbuf.at[c, 1 - core], out_hbm.at[core, c], send_sem.at[10], out_sem.at[1], cpeer).start()
 
-    lag4 = jnp.where(s >= LATE - 1, 4, LAG4)
-    stages = {0: (stage0, LAG0), 1: (stage1, 0), 2: (stage2, LAG2), 3: (stage3, LAG3), 4: (stage4, lag4)}
-
-    stage0(0)
-    if LAG0 == -2:
-        stage0(1)
-
     def tick(k, carry):
         @pl.when(k == LAG4)
         def _():
             wait_for(wo, load_sem.at[1])
             load_cot.wait()
 
-        for which in ORDER:
-            stage, lag = stages[which]
-
-            @pl.when((k >= lag) & (k < NC + lag))
-            def _(stage=stage, lag=lag):
+        def run(stage, lag, where=None):
+            now = (k >= lag) & (k < NC + lag)
+
+            @pl.when(now if where is None else now & where)
+            def _():
                 stage(k - lag)
 
+        for stage, lag in ((stage1, 0),):
+            run(stage, lag)
+        run(stage4, LAGP, s >= LATE - 1)
+        run(stage2, LAG2)
+        run(stage3, LAG3)
+        run(stage4, LAG4, s < LATE - 1)
         return carry
 
-    lax.fori_loop(0, NC + 4, tick, 0)
+    lax.fori_loop(0, NC + LAGP, tick, 0)
 
     over_rows = (((0,), (0,)), ((), ()))
     over_cols = (((1,), (1,)), ((), ()))
@@ -368,14 +357,18 @@
     def _():
         wait_for(outbuf, send_sem.at[8])
 
-    @pl.when((s >= LATE - 2) & (s < 6))
+    @pl.when((s >= LATE - 2) & (s < 6) & jnp.logical_not(odd))
     def _():
         wait_for(outbuf, send_sem.at[14])
 
+    @pl.when((s >= LATE - 2) & (s < 6) & odd)
+    def _():
+        wait_for(sct, send_sem.at[14])
+
     @pl.when((s >= LATE - 1) & (s < 7))
     def _():
         wait_for(wo.at[0], send_sem.at[11])
-        wait_for(vin.at[:, 0], send_sem.at[13])
+        wait_for(vin, send_sem.at[13])
 
     @pl.when(s >= LATE)
     def _():
@@ -383,8 +376,7 @@
 
     @pl.when((s >= LATE) & (s < 7) & jnp.logical_not(odd))
     def _():
-        wait_for(vin.at[:, pl.ds(0, Y - 1)], send_sem.at[15])
-        wait_for(vin.at[:, pl.ds(0, Y - 1)], send_sem.at[15])
+        wait_for(sct, send_sem.at[15])
 
     left_copy.wait()
     right_copy.wait()
@@ -440,7 +432,6 @@
             dma((2,)),
             dma((2,)),
             dma((NC,)),
-            dma((NC,)),
             dma((PIECES + 1,)),
             dma((16,)),
             dma((6,)),

time: 235 us -> 228 us (0.970)
  Pallas kernels: 228 us -> 221 us
    pallas_call x1, Pallas kernels: 228 us -> 221 us  [on_device(): pl.pallas_call(kernel, out_shape=(jax.ShapeDtypeStruct((2, NC, T, W), BF1...]
where the time goes in v5:
time: 228 us
  Pallas kernels  221 us (97%)
  local copies, waits for them, and re-layouts  5.96 us (3%)
    pallas_call x1, Pallas kernels, on_device(): pl.pallas_call(kernel, out_shape=(jax.ShapeDtypeStruct((2, NC, T, W), BF1...  221 us
    unnamed x7, local copies, waits for them, and re-layouts  5.96 us

profile of v5, /device:TPU:70, one launch (start us, length us, event | category | flops | bytes accessed | tf_op | source)
XLA Modules:
  0.0 227.9 jit_solution(6398454710622211286)
XLA Ops:
  0.6 221.3 %shard_map.94 = (bf16[2,16,32,1024]{3,2,1,0:T(8,128)(2,1)}, f32[1024,1024]{1,0:T(8,128)}, f32[64,1024]{1,0:T(8,128)}) custom-call(bf16[2,16,32,1024]{3,2,1,0:T(8,128)(2,1)} %bitcast.12, bf16[2,16,32,1024]{3,2,1,0:T(8,128)(2,1)} %bitcast.13, bf16[1,1024]{1,0:T(2,128)(2,1)} %gain_ref.1, bf16[1024,1024]{1,0:T(8,128)(2,1)} %bitcast.14, ...), custom_call_target="tpu_custom_call" | custom-call | tf_op jit(solution)/shard_map/pallas_call | solution.py:388
  221.9 0.0 copy-start
  222.0 3.2 %copy.13 = bf16[1,8,128,1024]{3,2,1,0:T(8,128)(2,1)} copy(bf16[1,8,128,1024]{3,2,1,0:T(8,128)(2,1)} %bitcast.11) | data formatting | bytes 4194304
  225.2 0.0 copy-done
  225.2 0.0 copy-start.1
  225.2 2.0 copy.14
  227.2 0.0 copy-done.1
  227.2 0.7 copy.15
Async XLA Ops:
  221.9 3.2 %copy-start = (f32[1024,1024]{1,0:T(8,128)S(1)}, f32[1024,1024]{1,0:T(8,128)}, u32[]{:S(2)}) copy-start(f32[1024,1024]{1,0:T(8,128)} %get-tuple-element.7) | copy-start | bytes 12582916
  225.2 2.0 copy-start.1
